TPU v7x, 32 devices: a whole 2x2x4 slice. The times are simulated.
32 devices in a mesh: panel: 4 (over y, x), tile: 8 (over z, core).
Axes of the slice: x: 2, y: 2, z: 4, core: 2. Of those that a mesh axis runs over, the one named last changes fastest.
Arguments:
- snapshots: bfloat16 [32, 64, 2, 512], P('panel', 'tile'), may hold values from -24 to 24
- beam_codes: int32 [32, 64], P(None, 'tile'), may hold values from 0 to 63
- panel_codes: int32 [32], replicated, may hold values from 0 to 63
- loading: float32 [32], P('panel'), may hold values from 1 to 10
Outputs:
- cancel: float32 [32, 62, 2], P('panel')
- beam_out: float32 [2, 512], P(None, 'tile')
All inputs are finite; a program needn't handle non-finite values.
Results may differ from a plain program's by a relative error of at most 0.0036.
Values may be sent and summed in bfloat16 or wider, within the bound.
A program may use at most 64 MiB of HBM per device.

v0:
```python
import functools
import math

import jax
import jax.numpy as jnp
from jax import lax
from jax.experimental import pallas as pl
from jax.experimental.pallas import tpu as pltpu
from jax.sharding import PartitionSpec as P

MESH = pl.DeviceIdType.MESH
LANES = 128
SUBS = 8
WIDE = 2
GRANT = 16 * 1024 * 1024
HIGH = lax.Precision.HIGHEST

phase_levels = 64
array_load = 1.0


def steering_rows(codes, total_tiles):
    angles = codes.astype(jnp.float32) * (2.0 * math.pi / phase_levels)
    cosine = jnp.cos(angles)
    sine = jnp.sin(angles)
    count_beams = codes.shape[0]
    count_tiles = codes.shape[1]
    real_rows = jnp.stack([cosine, sine], axis=-1).reshape(count_beams, 2 * count_tiles)
    imag_rows = jnp.stack([-sine, cosine], axis=-1).reshape(count_beams, 2 * count_tiles)
    table = jnp.stack([real_rows, imag_rows], axis=1).reshape(2 * count_beams, 2 * count_tiles)
    return (table / math.sqrt(total_tiles)).astype(jnp.bfloat16)


def solve_one(factor_one, right_one):
    return jax.scipy.linalg.cho_solve((factor_one, True), right_one)


def cancel_weights(covar):
    factor = jnp.linalg.cholesky(covar[:, 2:, 2:])
    return jax.vmap(solve_one)(factor, covar[:, 2:, :2])


def constraint_matrix(panel_codes):
    angles = panel_codes.astype(jnp.float32) * (2.0 * math.pi / phase_levels)
    cosine = jnp.cos(angles)
    sine = jnp.sin(angles)
    upper = jnp.stack([cosine, -sine], axis=-1)
    lower = jnp.stack([sine, cosine], axis=-1)
    return jnp.stack([upper, lower], axis=1).reshape(2 * panel_codes.shape[0], 2)


def array_weights(covar, constraint):
    factor = jnp.linalg.cholesky(covar)
    solved = jax.scipy.linalg.cho_solve((factor, True), constraint)
    gram = jnp.dot(constraint.T, solved, precision=HIGH)
    determinant = gram[0, 0] * gram[1, 1] - gram[0, 1] * gram[1, 0]
    inverse = (
        jnp.stack([jnp.stack([gram[1, 1], -gram[0, 1]]), jnp.stack([-gram[1, 0], gram[0, 0]])])
        / determinant
    )
    return jnp.dot(solved, inverse, precision=HIGH)


def plain_body(snapshots, beam_codes, panel_codes, loading):
    own_panels, own_tiles, _, snaps = snapshots.shape
    tile_count = lax.axis_size("tile")
    block_snaps = snaps // tile_count
    table = steering_rows(beam_codes, own_tiles * tile_count)
    samples = snapshots.reshape(own_panels, 2 * own_tiles, snaps)
    partial_value = jnp.einsum("bk,pks->pbs", table, samples, preferred_element_type=jnp.float32)
    totals = lax.psum(partial_value, "tile")
    summed = jnp.einsum("pis,pjs->pij", totals, totals, precision=HIGH)
    start = lax.axis_index("tile") * block_snaps
    beams = lax.dynamic_slice_in_dim(totals, start, block_snaps, 2)
    identity = jnp.eye(beams.shape[1], dtype=jnp.float32)
    covar = summed / snaps + loading[:, None, None] * identity[None, :, :]
    cancel = cancel_weights(covar)
    outputs = beams[:, :2, :] - jnp.einsum("pak,pas->pks", cancel, beams[:, 2:, :], precision=HIGH)
    gathered = lax.all_gather(outputs, "panel", axis=0, tiled=True)
    flat = gathered.reshape(gathered.shape[0] * 2, block_snaps)
    array_sum = lax.psum(jnp.dot(flat, flat.T, precision=HIGH), "tile")
    array_covar = array_sum / snaps + array_load * jnp.eye(flat.shape[0], dtype=jnp.float32)
    weights = array_weights(array_covar, constraint_matrix(panel_codes))
    beam_out = jnp.dot(weights.T, flat, precision=HIGH) * math.sqrt(flat.shape[0] // 2)
    return (cancel, beam_out)


def iota(shape, dim):
    return lax.broadcasted_iota(jnp.int32, shape, dim)


def cos_code(code):
    code = code & (phase_levels - 1)
    eighth = phase_levels // 8
    quarter = phase_levels // 4
    quadrant = ((code + eighth) >> 4) & 3
    rest = code - (((code + eighth) >> 4) * quarter)
    x = rest.astype(jnp.float32) * (2.0 * math.pi / phase_levels)
    y = x * x
    cosine = 1.0 + y * (-0.5 + y * (1 / 24 + y * (-1 / 720 + y * (1 / 40320 - y * (1 / 3628800)))))
    sine = x * (1.0 + y * (-1 / 6 + y * (1 / 120 + y * (-1 / 5040 + y * (1 / 362880)))))
    odd = (quadrant & 1) == 1
    flip = jnp.where((quadrant == 1) | (quadrant == 2), -1.0, 1.0)
    return jnp.where(odd, sine, cosine) * flip


def contract(a, b, dims, precision=HIGH):
    return lax.dot_general(a, b, (dims, ((), ())), precision=precision, preferred_element_type=jnp.float32)


def spread(value, row):
    return jnp.broadcast_to(value[row : row + 1], value.shape)


def lane_of(value, where_lane):
    return jnp.take_along_axis(value, jnp.broadcast_to(where_lane, value.shape), axis=1)


def tree(terms):
    terms = list(terms)
    while len(terms) > 1:
        terms = [sum(terms[i : i + 2][1:], terms[i]) for i in range(0, len(terms), 2)]
    return terms[0]


def eliminate(rows, pivots, wide, parts):
    shape = rows[0].shape
    sub, lane = iota(shape, 0), iota(shape, 1)
    span = shape[1] // parts
    first = lane // span * span
    count = len(rows)
    rows = list(rows)

    def pick(value, c):
        if parts > 1:
            return lane_of(value, first + c)
        return jnp.broadcast_to(jnp.sum(jnp.where(lane == c, value, 0.0), axis=1, keepdims=True), shape)

    for base in range(0, count, wide):
        cols = list(range(base * SUBS, min((base + wide) * SUBS, pivots)))
        outer = [(base + wide + k) % count for k in range(count - wide)]
        inner = rows[base : base + wide]
        diag = {c: [pick(value, c) for value in inner] for c in cols}
        factor = {c: [pick(rows[g], c) for g in outer] for c in cols}
        for c in cols[::2]:
            g, s = c // SUBS - base, c % SUBS
            a, b = spread(diag[c][g], s), spread(diag[c + 1][g], s)
            e, d = spread(diag[c][g], s + 1), spread(diag[c + 1][g], s + 1)
            scale = 1.0 / (a * d - b * e)
            top, bottom = sub == s, sub == s + 1
            left = [x * d - y * e for x, y in zip(diag[c], diag[c + 1])]
            right = [y * a - x * b for x, y in zip(diag[c], diag[c + 1])]
            left[g] = jnp.where(top, -d, jnp.where(bottom, e, left[g]))
            right[g] = jnp.where(top, b, jnp.where(bottom, -a, right[g]))
            left = [value * scale for value in left]
            right = [value * scale for value in right]

            def reduce(values):
                row0, row1 = spread(values[g], s), spread(values[g], s + 1)
                kept = list(values)
                kept[g] = jnp.where(top | bottom, 0.0, kept[g])
                return [v - l * row0 - r * row1 for v, l, r in zip(kept, left, right)]

            for k in cols:
                if k > c + 1:
                    diag[k] = reduce(diag[k])
            inner = reduce(inner)
        rows[base : base + wide] = inner
        pivot = {c: spread(inner[c // SUBS - base], c % SUBS) for c in cols}
        for q, g in enumerate(outer):
            rows[g] = rows[g] - tree(factor[c][q] * pivot[c] for c in cols)
    return rows


def gather_kernel(
    sizes, loading_in, snaps_in, codes_in, panel_codes_in, flat, cancels, steer,
    loading, panel_codes, own, got, codes_own, codes_got,
    local_sem, send_a, recv_a, send_c, recv_c, send_f, recv_f, send_w, recv_w,
):
    panel_count, tile_count, total_panels = sizes
    own_panels, own_tiles, _, snaps = snaps_in.shape
    total_tiles = own_tiles * tile_count
    beams_count = codes_in.shape[1]
    width = 2 * beams_count
    chunks = snaps // LANES
    owners = tile_count // 2
    pi, ti = lax.axis_index("panel"), lax.axis_index("tile")
    spare = tile_count - 4
    row = jnp.where(ti == spare, owners - 1, lax.div(ti, 2))
    seat = lambda q: jnp.where(q < owners - 1, 2 * q + 1, spare)
    owner = ti == seat(row)
    mates = [jnp.where(k >= ti, k + 1, k) for k in range(tile_count - 1)]
    panels = [jnp.where(k >= pi, k + 1, k) for k in range(panel_count - 1)]
    seats = []
    for k in range(owners):
        last = (k + owners - 1) % owners
        right = jnp.where(ti < tile_count - 2, k, last)
        seats.append(jnp.where(ti < tile_count // 2, owners - 1 - k, right))

    barrier = pltpu.get_barrier_semaphore()

    @pl.when(owner)
    def _():
        for t in mates:
            pl.semaphore_signal(barrier, inc=1, device_id=(pi, t), device_id_type=MESH)

    for p in panels:
        pl.semaphore_signal(barrier, inc=1, device_id=(p, ti), device_id_type=MESH)
    loads = [
        pltpu.make_async_copy(source, target, local_sem.at[index])
        for index, (source, target) in enumerate((
            (snaps_in, own),
            (codes_in, codes_own),
            (loading_in, loading),
            (panel_codes_in, panel_codes),
        ))
    ]
    for load in loads:
        load.start()
    for load in loads[:2]:
        load.wait()
    pl.semaphore_wait(barrier, panel_count - 1 + owners - jnp.where(owner, 1, 0))

    def code_to(q):
        return pltpu.make_async_remote_copy(
            codes_own, codes_got.at[ti], send_c, recv_c, device_id=(pi, seat(q)), device_id_type=MESH
        )

    def bulk_to(q):
        return pltpu.make_async_remote_copy(
            own.at[pl.ds(2 * q, 2)], got.at[ti], send_a, recv_a,
            device_id=(pi, seat(q)), device_id_type=MESH,
        )

    for q in seats:
        pl.when(seat(q) != ti)(code_to(q).start)
    for q in seats:
        pl.when(seat(q) != ti)(bulk_to(q).start)

    for load in loads[2:]:
        load.wait()
    order = 2 * total_panels
    quarter = phase_levels // 4
    code_row = jnp.broadcast_to(panel_codes[...], (order, total_panels))
    own_code = jnp.where(iota((order, total_panels), 1) == lax.rem(iota((order, total_panels), 0), total_panels), code_row, 0)
    code_col = jnp.broadcast_to(jnp.sum(own_code, axis=1, keepdims=True), (order, LANES))
    lower = iota((order, LANES), 0) >= total_panels
    steer[0] = cos_code(code_col + jnp.where(lower, -quarter, 0))
    steer[1] = cos_code(code_col + jnp.where(lower, 0, quarter))

    mine = pi * own_panels + 2 * row
    me = pi * owners + row
    span = 2 * panel_count
    rank = lax.div(ti, 2) * span + 2 * pi + lax.rem(ti, 2)
    targets = []
    for k in range(panel_count * tile_count - 1):
        n = jnp.where(k >= rank, k + 1, k)
        within = lax.rem(n, span)
        targets.append((lax.div(within, 2), 2 * lax.div(n, span) + lax.rem(within, 2)))

    def flat_to(to):
        return pltpu.make_async_remote_copy(
            flat.at[pl.ds(mine, 2)], flat.at[pl.ds(mine, 2)], send_f, recv_f,
            device_id=to, device_id_type=MESH,
        )

    def cancel_to(t):
        return pltpu.make_async_remote_copy(
            cancels.at[pl.ds(2 * row, 2)], cancels.at[pl.ds(2 * row, 2)], send_w, recv_w,
            device_id=(pi, t), device_id_type=MESH,
        )

    def total_of(ref, count, send, recv):
        part = ref if count == ref.shape[0] else ref.at[pl.ds(0, count)]
        return pltpu.make_async_remote_copy(part, part, send, recv, device_id=(pi, mates[0]), device_id_type=MESH)

    def arrived(ref, count, send, recv):
        total_of(ref, count, send, recv).wait_recv()

    def left_here(ref, count, send, recv):
        while count:
            now = min(count, ref.shape[0])
            total_of(ref, now, send, recv).wait_send()
            count -= now

    @pl.when(owner)
    def _():
        arrived(codes_got, tile_count - 1, send_c, recv_c)
        codes_got[ti] = codes_own[...]
        codes_all = codes_got[...].reshape(total_tiles, beams_count).astype(jnp.float32).astype(jnp.bfloat16)
        beam_of = lax.rem(iota((width, beams_count), 0) + 2, width) >> 1
        b_rows = (beam_of == iota((width, beams_count), 1)).astype(jnp.float32).astype(jnp.bfloat16)
        k_cols = (iota((total_tiles, 2 * total_tiles), 1) >> 1) == iota((total_tiles, 2 * total_tiles), 0)
        tall = contract(b_rows, codes_all, ((1,), (1,)), None)
        wide = contract(tall.astype(jnp.bfloat16), k_cols.astype(jnp.float32).astype(jnp.bfloat16), ((1,), (0,)), None)
        code = (wide + 0.5).astype(jnp.int32)
        turn = (iota(code.shape, 0) & 1) - (iota(code.shape, 1) & 1)
        table = (cos_code(code + quarter * turn) / math.sqrt(total_tiles)).astype(jnp.bfloat16)

        got[ti] = own[pl.ds(2 * row, 2)]
        arrived(got, tile_count - 1, send_a, recv_a)
        beams = [
            contract(table, got[:, h].reshape(2 * total_tiles, snaps), ((1,), (0,)), None) for h in range(2)
        ]
        both = jnp.concatenate(beams, axis=0)
        covar = contract(both, both, ((1,), (1,)))
        square = (width, LANES)
        lane, r_of = iota(square, 1), iota(square, 0)
        left = lane < width
        full = jnp.where(left, covar[:width], covar[width:]) / snaps
        load_lane = jnp.where(left, loading[2 * row], loading[2 * row + 1])
        full = full + jnp.where(lax.rem(lane, width) == r_of, load_lane, 0.0)
        groups = eliminate([full[r : r + SUBS] for r in range(0, width, SUBS)], width - 2, WIDE, 2)
        turned = jnp.concatenate(groups, axis=0).T
        for h in range(2):
            cancels[2 * row + h] = turned[(h + 1) * width - 2 : (h + 1) * width, : width - 2]
        sub, lanes = iota((SUBS, LANES), 0), iota((SUBS, LANES), 1)
        for h in range(2):
            weigh = []
            for k in range(2):
                cols = [-lane_of(value, jnp.full((SUBS, LANES), h * width + width - 2 + k, jnp.int32)) for value in groups]
                cols[-1] = jnp.where(sub < SUBS - 2, cols[-1], jnp.where(sub == SUBS - 2 + k, 1.0, 0.0))
                weigh.append(cols)
            placed = jnp.zeros((SUBS, LANES), jnp.float32)
            for j in range(chunks):
                for k in range(2):
                    total = tree(
                        weigh[k][g] * beams[h][g * SUBS : (g + 1) * SUBS, j * LANES : (j + 1) * LANES]
                        for g in range(width // SUBS)
                    )
                    line = jnp.broadcast_to(jnp.sum(total, axis=0, keepdims=True), (SUBS, LANES))
                    placed = jnp.where(sub == 2 * j + k, line, placed)
            flat[mine + h] = placed
        for to in targets[:2]:
            flat_to(to).start()
        for t in mates:
            cancel_to(t).start()
        for to in targets[2:]:
            flat_to(to).start()

    @pl.when(owner)
    def _():
        arrived(flat, total_panels - 2, send_f, recv_f)
        arrived(cancels, own_panels - 2, send_w, recv_w)
        left_here(codes_got, owners - 1, send_c, recv_c)
        left_here(got, owners - 1, send_a, recv_a)
        left_here(flat, 2 * len(targets), send_f, recv_f)
        left_here(cancels, 2 * len(mates), send_w, recv_w)

    @pl.when(jnp.logical_not(owner))
    def _():
        arrived(flat, total_panels, send_f, recv_f)
        arrived(cancels, own_panels, send_w, recv_w)
        left_here(codes_got, owners, send_c, recv_c)
        left_here(got, owners, send_a, recv_a)


def array_kernel(sizes, flat, cancels, steer, cancel_out, beam_out, out_sem):
    tile_count, total_panels, snaps = sizes
    order = 2 * total_panels
    chunks = snaps // LANES
    count = order // SUBS
    ti = lax.axis_index("tile")
    store = pltpu.make_async_copy(cancels, cancel_out, out_sem)
    store.start()
    parts = [jnp.concatenate([flat[:, 2 * j, :], flat[:, 2 * j + 1, :]], axis=0) for j in range(chunks)]
    joined = jnp.concatenate(parts, axis=1)
    square = (order, LANES)
    lane, r_of = iota(square, 1), iota(square, 0)
    covar = contract(joined, joined, ((1,), (1,))) / snaps
    covar = covar + jnp.where(iota((order, order), 0) == iota((order, order), 1), array_load, 0.0)
    full = jnp.concatenate([covar, jnp.zeros((order, LANES - order), jnp.float32)], axis=1)
    full = jnp.where(lane == order, steer[0], jnp.where(lane == order + 1, steer[1], full))
    block = snaps // tile_count
    per = LANES // block
    chunk, spot = lax.div(ti, per), lax.rem(ti, per)
    mine = parts[0]
    for j in range(1, chunks):
        mine = jnp.where(chunk == j, parts[j], mine)
    turned = mine
    for j in range(1, per):
        turned = jnp.where(spot == j, pltpu.roll(mine, LANES - j * block, 1), turned)
    groups = eliminate([full[r : r + SUBS] for r in range(0, order, SUBS)], order, WIDE, 1)
    solved = [[lane_of(value, jnp.full((SUBS, LANES), order + k, jnp.int32)) for value in groups] for k in range(2)]
    cut = lambda value, g: value[g * SUBS : (g + 1) * SUBS]
    inner = lambda cols, value: jnp.sum(tree(cols[g] * cut(value, g) for g in range(count)), axis=0, keepdims=True)
    s0, s1 = inner(solved[0], turned), inner(solved[1], turned)
    g00, g01 = inner(solved[0], steer[0]), inner(solved[1], steer[0])
    g10, g11 = inner(solved[0], steer[1]), inner(solved[1], steer[1])
    scale = math.sqrt(total_panels) / (g00 * g11 - g01 * g10)
    beam_out[0:1, :] = ((g11 * s0 - g10 * s1) * scale)[:, :block]
    beam_out[1:2, :] = ((g00 * s1 - g01 * s0) * scale)[:, :block]
    store.wait()


def fused_body(panel_count, tile_count, snapshots, beam_codes, panel_codes, loading):
    own_panels, own_tiles, _, snaps = snapshots.shape
    beams_count = beam_codes.shape[0]
    total_panels = own_panels * panel_count
    owners = tile_count // 2
    dma = pltpu.SemaphoreType.DMA
    any_space = pl.BlockSpec(memory_space=pl.ANY)
    vmem = pl.BlockSpec(memory_space=pltpu.VMEM)
    aux = 2 * beams_count - 2
    flat, cancels, steer = pl.pallas_call(
        functools.partial(gather_kernel, (panel_count, tile_count, total_panels)),
        out_shape=(
            pltpu.VMEM((total_panels, 2 * snaps // LANES, LANES), jnp.float32),
            pltpu.VMEM((own_panels, 2, aux), jnp.float32),
            pltpu.VMEM((2, 2 * total_panels, LANES), jnp.float32),
        ),
        in_specs=[any_space] * 4,
        out_specs=(vmem, vmem, vmem),
        scratch_shapes=[
            pltpu.SMEM(loading.shape, loading.dtype),
            pltpu.VMEM((1, total_panels), jnp.int32),
            pltpu.VMEM(snapshots.shape, snapshots.dtype),
            pltpu.VMEM((tile_count, 2, own_tiles, 2, snaps), snapshots.dtype),
            pltpu.VMEM((own_tiles, beams_count), jnp.int32),
            pltpu.VMEM((tile_count, own_tiles, beams_count), jnp.int32),
            dma((4,)),
            dma,
            dma,
            dma,
            dma,
            dma,
            dma,
            dma,
            dma,
        ],
        compiler_params=pltpu.CompilerParams(collective_id=0, has_side_effects=True),
        name="panels",
    )(loading, snapshots, beam_codes.T, panel_codes.reshape(1, -1))
    cancel_t, beam_out = pl.pallas_call(
        functools.partial(array_kernel, (tile_count, total_panels, snaps)),
        out_shape=(
            jax.ShapeDtypeStruct((own_panels, 2, aux), jnp.float32),
            jax.ShapeDtypeStruct((2, snaps // tile_count), jnp.float32),
        ),
        in_specs=[vmem] * 3,
        out_specs=(any_space, vmem),
        scratch_shapes=[dma],
        compiler_params=pltpu.CompilerParams(vmem_limit_bytes=GRANT),
        name="array",
    )(flat, cancels, steer)
    return (jnp.transpose(cancel_t, (0, 2, 1)), beam_out)


def body(mesh_shape, snapshots, beam_codes, panel_codes, loading):
    panel_count, tile_count = mesh_shape
    own_panels, own_tiles, _, snaps = snapshots.shape
    block = snaps // tile_count
    fits = (
        own_panels == tile_count
        and tile_count % 2 == 0
        and tile_count >= 4
        and own_tiles % SUBS == 0
        and 4 * beam_codes.shape[0] == LANES
        and (2 * own_panels * panel_count) % (WIDE * SUBS) == 0
        and 2 * own_panels * panel_count + 2 <= LANES
        and 2 * snaps == SUBS * LANES
        and block <= LANES
        and LANES % block == 0
    )
    if not fits:
        return plain_body(snapshots, beam_codes, panel_codes, loading)
    return fused_body(panel_count, tile_count, snapshots, beam_codes, panel_codes, loading)


def solution(mesh):
    placed = (P("panel", "tile", None, None), P(None, "tile"), P(), P("panel"))
    return jax.shard_map(
        functools.partial(body, (mesh.shape["panel"], mesh.shape["tile"])),
        mesh=mesh,
        in_specs=placed,
        out_specs=(P("panel", None, None), P(None, "tile")),
        check_vma=False,
    )
```

profile of v0, /device:TPU:0, one launch (start us, length us, event | category | flops | bytes accessed | tf_op | source)
XLA Modules:
  0.0 18.0 jit_solution(8071854798142638983)
XLA Ops:
  0.6 15.3 %panels.1 = (f32[32,8,128]{2,1,0:T(8,128)S(1)}, f32[8,2,62]{2,1,0:T(2,128)S(1)}, f32[2,64,128]{2,1,0:T(8,128)S(1)}) custom-call(f32[8]{0:T(128)} %loading_in.1, bf16[8,8,2,512]{3,2,1,0:T(2,128)(2,1)} %snaps_in.1, s32[8,32]{1,0:T(8,128)} %bitcast.3, s32[1,32]{1,0:T(1,128)} %bitcast.4), custom_call_target="tpu_custom_call" | custom-call | tf_op jit(solution)/shard_map/panels/pallas_call | solution.py:405
  15.9 2.0 %array.1 = (f32[8,2,62]{2,1,0:T(2,128)}, f32[2,64]{1,0:T(2,128)}) custom-call(f32[32,8,128]{2,1,0:T(8,128)S(1)} %get-tuple-element.7.flat, f32[8,2,62]{2,1,0:T(2,128)S(1)} %get-tuple-element.8.cancels, f32[2,64,128]{2,1,0:T(8,128)S(1)} %get-tuple-element.9.steer), custom_call_target="tpu_custom_call" | custom-call | tf_op jit(solution)/shard_map/array/pallas_call | solution.py:434
where the time goes:
time: 18.1 us; the launch traced here: 18 us
  Pallas kernels  17.3 us (96%)
  between operations  0.64 us (4%)
    pallas_call x1, Pallas kernels, fused_body(): pl.pallas_call(functools.partial(gather_kernel, (panel_count, tile_count,...  15.3 us
    pallas_call x1, Pallas kernels, fused_body(): pl.pallas_call(functools.partial(array_kernel, (tile_count, total_panels,...  2.03 us

commit v1 on v0

--- a/solution.py
+++ b/solution.py
@@ -106,6 +106,27 @@
 
 def contract(a, b, dims, precision=HIGH):
     return lax.dot_general(a, b, (dims, ((), ())), precision=precision, preferred_element_type=jnp.float32)
+
+
+def gram(value):
+    count = value.shape[0]
+    half = jnp.bfloat16
+    high = value.astype(half)
+    rest = value - high.astype(jnp.float32)
+    middle = rest.astype(half)
+    low = (rest - middle.astype(jnp.float32)).astype(half)
+    across = ((1,), (1,))
+    if count % LANES == 0:
+        first = contract(jnp.concatenate([high, middle, low], axis=0), jnp.concatenate([high, middle], axis=0), across, None)
+        third = contract(high, low, across, None)
+        row = lambda k: first[k * count : (k + 1) * count]
+        small = row(2)[:, :count] + third + row(1)[:, count:]
+        return small + (row(1)[:, :count] + row(0)[:, count:]) + row(0)[:, :count]
+    first = contract(jnp.concatenate([high, middle, low], axis=0), high, across, None)
+    second = contract(jnp.concatenate([high, middle], axis=0), middle, across, None)
+    third = contract(high, low, across, None)
+    small = first[2 * count :] + third + second[count:]
+    return small + (first[count : 2 * count] + second[:count]) + first[:count]
 
 
 def spread(value, row):
@@ -199,25 +220,26 @@
 
     barrier = pltpu.get_barrier_semaphore()
 
-    @pl.when(owner)
-    def _():
-        for t in mates:
-            pl.semaphore_signal(barrier, inc=1, device_id=(pi, t), device_id_type=MESH)
-
-    for p in panels:
-        pl.semaphore_signal(barrier, inc=1, device_id=(p, ti), device_id_type=MESH)
     loads = [
         pltpu.make_async_copy(source, target, local_sem.at[index])
         for index, (source, target) in enumerate((
-            (snaps_in, own),
             (codes_in, codes_own),
             (loading_in, loading),
             (panel_codes_in, panel_codes),
         ))
     ]
-    for load in loads:
+    parts = [pltpu.make_async_copy(snaps_in, own, local_sem.at[len(loads)])]
+    for load in parts + loads:
         load.start()
-    for load in loads[:2]:
+
+    @pl.when(owner)
+    def _():
+        for t in mates:
+            pl.semaphore_signal(barrier, inc=1, device_id=(pi, t), device_id_type=MESH)
+
+    for p in panels:
+        pl.semaphore_signal(barrier, inc=1, device_id=(p, ti), device_id_type=MESH)
+    for load in parts + loads[:1]:
         load.wait()
     pl.semaphore_wait(barrier, panel_count - 1 + owners - jnp.where(owner, 1, 0))
 
@@ -237,7 +259,7 @@
     for q in seats:
         pl.when(seat(q) != ti)(bulk_to(q).start)
 
-    for load in loads[2:]:
+    for load in loads[1:]:
         load.wait()
     order = 2 * total_panels
     quarter = phase_levels // 4
@@ -303,7 +325,7 @@
             contract(table, got[:, h].reshape(2 * total_tiles, snaps), ((1,), (0,)), None) for h in range(2)
         ]
         both = jnp.concatenate(beams, axis=0)
-        covar = contract(both, both, ((1,), (1,)))
+        covar = gram(both)
         square = (width, LANES)
         lane, r_of = iota(square, 1), iota(square, 0)
         left = lane < width
@@ -367,7 +389,7 @@
     joined = jnp.concatenate(parts, axis=1)
     square = (order, LANES)
     lane, r_of = iota(square, 1), iota(square, 0)
-    covar = contract(joined, joined, ((1,), (1,))) / snaps
+    covar = gram(joined) / snaps
     covar = covar + jnp.where(iota((order, order), 0) == iota((order, order), 1), array_load, 0.0)
     full = jnp.concatenate([covar, jnp.zeros((order, LANES - order), jnp.float32)], axis=1)
     full = jnp.where(lane == order, steer[0], jnp.where(lane == order + 1, steer[1], full))

time: 18.1 us -> 18.1 us (level)
  no operation moved by 1% of the time
where the time goes in v1:
time: 18.1 us; the launch traced here: 17.9 us
  Pallas kernels  17.3 us (96%)
  between operations  0.64 us (4%)
    pallas_call x1, Pallas kernels, fused_body(): pl.pallas_call(functools.partial(gather_kernel, (panel_count, tile_count,...  15.3 us
    pallas_call x1, Pallas kernels, fused_body(): pl.pallas_call(functools.partial(array_kernel, (tile_count, total_panels,...  2 us

profile of v1, /device:TPU:0, one launch (start us, length us, event | category | flops | bytes accessed | tf_op | source)
XLA Modules:
  0.0 17.9 jit_solution(263908923839106102)
XLA Ops:
  0.6 15.3 %panels.1 = (f32[32,8,128]{2,1,0:T(8,128)S(1)}, f32[8,2,62]{2,1,0:T(2,128)S(1)}, f32[2,64,128]{2,1,0:T(8,128)S(1)}) custom-call(f32[8]{0:T(128)} %loading_in.1, bf16[8,8,2,512]{3,2,1,0:T(2,128)(2,1)} %snaps_in.1, s32[8,32]{1,0:T(8,128)} %bitcast.3, s32[1,32]{1,0:T(1,128)} %bitcast.4), custom_call_target="tpu_custom_call" | custom-call | tf_op jit(solution)/shard_map/panels/pallas_call | solution.py:427
  15.9 2.0 %array.1 = (f32[8,2,62]{2,1,0:T(2,128)}, f32[2,64]{1,0:T(2,128)}) custom-call(f32[32,8,128]{2,1,0:T(8,128)S(1)} %get-tuple-element.7.flat, f32[8,2,62]{2,1,0:T(2,128)S(1)} %get-tuple-element.8.cancels, f32[2,64,128]{2,1,0:T(8,128)S(1)} %get-tuple-element.9.steer), custom_call_target="tpu_custom_call" | custom-call | tf_op jit(solution)/shard_map/array/pallas_call | solution.py:456

commit v2 on v1

--- a/solution.py
+++ b/solution.py
@@ -144,7 +144,7 @@
     return terms[0]
 
 
-def eliminate(rows, pivots, wide, parts):
+def eliminate(rows, pivots, wide, parts, sides=()):
     shape = rows[0].shape
     sub, lane = iota(shape, 0), iota(shape, 1)
     span = shape[1] // parts
@@ -161,8 +161,14 @@
         cols = list(range(base * SUBS, min((base + wide) * SUBS, pivots)))
         outer = [(base + wide + k) % count for k in range(count - wide)]
         inner = rows[base : base + wide]
-        diag = {c: [pick(value, c) for value in inner] for c in cols}
-        factor = {c: [pick(rows[g], c) for g in outer] for c in cols}
+        diag, factor = {}, {}
+        for c in cols:
+            diag[c] = [pick(value, c) for value in inner]
+            factor[c] = [pick(rows[g], c) for g in outer]
+        ending = bool(sides) and base + wide >= count
+        if ending:
+            rest = {c: [pick(rows[g], c) for g in outer] for c in sides}
+            diag.update({c: [pick(value, c) for value in inner] for c in sides})
         for c in cols[::2]:
             g, s = c // SUBS - base, c % SUBS
             a, b = spread(diag[c][g], s), spread(diag[c + 1][g], s)
@@ -182,10 +188,19 @@
                 kept[g] = jnp.where(top | bottom, 0.0, kept[g])
                 return [v - l * row0 - r * row1 for v, l, r in zip(kept, left, right)]
 
-            for k in cols:
+            for k in diag:
                 if k > c + 1:
                     diag[k] = reduce(diag[k])
-            inner = reduce(inner)
+            if not ending:
+                inner = reduce(inner)
+        if ending:
+            solved = []
+            for k in sides:
+                pivot = {c: spread(diag[k][c // SUBS - base], c % SUBS) for c in cols}
+                found = {g: rest[k][q] - tree(factor[c][q] * pivot[c] for c in cols) for q, g in enumerate(outer)}
+                found.update({base + g: value for g, value in enumerate(diag[k])})
+                solved.append([found[g] for g in range(count)])
+            return solved
         rows[base : base + wide] = inner
         pivot = {c: spread(inner[c // SUBS - base], c % SUBS) for c in cols}
         for q, g in enumerate(outer):
@@ -402,8 +417,7 @@
     turned = mine
     for j in range(1, per):
         turned = jnp.where(spot == j, pltpu.roll(mine, LANES - j * block, 1), turned)
-    groups = eliminate([full[r : r + SUBS] for r in range(0, order, SUBS)], order, WIDE, 1)
-    solved = [[lane_of(value, jnp.full((SUBS, LANES), order + k, jnp.int32)) for value in groups] for k in range(2)]
+    solved = eliminate([full[r : r + SUBS] for r in range(0, order, SUBS)], order, WIDE, 1, (order, order + 1))
     cut = lambda value, g: value[g * SUBS : (g + 1) * SUBS]
     inner = lambda cols, value: jnp.sum(tree(cols[g] * cut(value, g) for g in range(count)), axis=0, keepdims=True)
     s0, s1 = inner(solved[0], turned), inner(solved[1], turned)

time: 18.1 us -> 18.1 us (level)
  no operation moved by 1% of the time
where the time goes in v2:
time: 18.1 us; the launch traced here: 17.9 us
  Pallas kernels  17.3 us (96%)
  between operations  0.64 us (4%)
    pallas_call x1, Pallas kernels, fused_body(): pl.pallas_call(functools.partial(gather_kernel, (panel_count, tile_count,...  15.3 us
    pallas_call x1, Pallas kernels, fused_body(): pl.pallas_call(functools.partial(array_kernel, (tile_count, total_panels,...  1.98 us

profile of v2, /device:TPU:0, one launch (start us, length us, event | category | flops | bytes accessed | tf_op | source)
XLA Modules:
  0.0 17.9 jit_solution(4816441670840274339)
XLA Ops:
  0.6 15.3 %panels.1 = (f32[32,8,128]{2,1,0:T(8,128)S(1)}, f32[8,2,62]{2,1,0:T(2,128)S(1)}, f32[2,64,128]{2,1,0:T(8,128)S(1)}) custom-call(f32[8]{0:T(128)} %loading_in.1, bf16[8,8,2,512]{3,2,1,0:T(2,128)(2,1)} %snaps_in.1, s32[8,32]{1,0:T(8,128)} %bitcast.3, s32[1,32]{1,0:T(1,128)} %bitcast.4), custom_call_target="tpu_custom_call" | custom-call | tf_op jit(solution)/shard_map/panels/pallas_call | solution.py:441
  15.9 2.0 %array.1 = (f32[8,2,62]{2,1,0:T(2,128)}, f32[2,64]{1,0:T(2,128)}) custom-call(f32[32,8,128]{2,1,0:T(8,128)S(1)} %get-tuple-element.7.flat, f32[8,2,62]{2,1,0:T(2,128)S(1)} %get-tuple-element.8.cancels, f32[2,64,128]{2,1,0:T(8,128)S(1)} %get-tuple-element.9.steer), custom_call_target="tpu_custom_call" | custom-call | tf_op jit(solution)/shard_map/array/pallas_call | solution.py:470
